TPU v7x, 32 devices: a whole 2x2x4 slice. The times are simulated.
32 devices in a mesh: sample: 2 (over y), gz: 4 (over x, core), gy: 4 (over z).
Axes of the slice: x: 2, y: 2, z: 4, core: 2. Of those that a mesh axis runs over, the one named last changes fastest.
Arguments:
- right_side: float32 [64, 64, 256], P(('sample', 'gz'), 'gy'), parts along dimension 0, may hold values from -8 to 8
- labels: int32 [8, 8, 32], P(('sample', 'gz'), 'gy'), parts along dimension 0, may hold values from 0 to 7
- region_coeff: float32 [16], P('sample'), parts along dimension 0, may hold values from 0.2 to 5
- shift_index: int32 [16], P('sample'), parts along dimension 0, may hold values from 0 to 15
- shift_table: float32 [16], replicated, may hold values from 0.1 to 4
- time_step: float32 [2], P('sample'), parts along dimension 0, may hold values from 0.3 to 1
- block_inverse: float32 [8, 128, 128], replicated, as said below
Outputs:
- solution: float32 [8, 64, 64, 256], P(None, ('sample', 'gz'), 'gy'), parts along dimension 1
- residual: float32 [8, 64, 64, 256], P(None, ('sample', 'gz'), 'gy'), parts along dimension 1
There are 2 independent parts, one for each index of `sample`. A program takes and returns all parts, laid end to end along the dimension named above; an argument that names none is the same for every part. Nothing has to cross between parts.
Inputs may be any that keep to these rules, and one draw needn't show every extreme that they name: `shift_index`: a table row for each system. `labels`: a region for each block. `block_inverse`: each block is symmetric and positive definite.
All inputs are finite; a program needn't handle non-finite values.
Results may differ from a plain program's by a relative error of at most 0.00022.
Values sent between devices are 32-bit elements; how exact they have to be, the bound alone decides.
A program may use at most 64 MiB of HBM per device.

v0:
```python
import jax
import jax.numpy as jnp
from jax import lax
from jax.sharding import PartitionSpec as P

SHIFTS = 8
ITERS = 2
BLOCK = 128
NEIGHBOURS = [
    (step_z, step_y, step_x, 0.5 ** (abs(step_z) + abs(step_y) + abs(step_x) - 1))
    for step_z in (-1, 0, 1)
    for step_y in (-1, 0, 1)
    for step_x in (-1, 0, 1)
    if (step_z, step_y, step_x) != (0, 0, 0)
]


def padded_2(block, sides, width):
    for axis, dim in sides:
        count = lax.axis_size(axis)
        forward = [(i, i + 1) for i in range(count - 1)]
        backward = [(target, source) for source, target in forward]
        low = lax.ppermute(
            lax.slice_in_dim(block, block.shape[dim] - width, None, axis=dim), axis, forward
        )
        high = lax.ppermute(lax.slice_in_dim(block, 0, width, axis=dim), axis, backward)
        block = jnp.concatenate([low, block, high], axis=dim)
    return block


def cell_values(labels, region_coeff):
    picked = jnp.where(labels[..., None] == jnp.arange(region_coeff.shape[0]), region_coeff, 0.0)
    table = jnp.sum(picked, axis=-1)
    return jnp.repeat(jnp.repeat(jnp.repeat(table, 8, 0), 8, 1), 8, 2)


def stencil(field, padded, conductivity, padded_cond):
    depth, rows, width = (field.shape[-3], field.shape[-2], field.shape[-1])
    total = jnp.zeros_like(field)
    for step_z, step_y, step_x, weight in NEIGHBOURS:
        beside = padded[
            ...,
            1 + step_z : 1 + step_z + depth,
            1 + step_y : 1 + step_y + rows,
            1 + step_x : 1 + step_x + width,
        ]
        cond_beside = padded_cond[
            1 + step_z : 1 + step_z + depth,
            1 + step_y : 1 + step_y + rows,
            1 + step_x : 1 + step_x + width,
        ]
        total = total + weight * 0.5 * (conductivity + cond_beside) * (field - beside)
    return total


def extend_field(field):
    extended = padded_2(field, (("gz", 1), ("gy", 2)), 1)
    return jnp.pad(extended, ((0, 0), (0, 0), (0, 0), (1, 1)))


def global_sum(values):
    row_sum = lax.psum(values, "gy")
    return lax.psum(row_sum, "gz")


def precondition(residual, block_inverse):
    shape = residual.shape
    blocks = residual.reshape(shape[0], shape[1], shape[2], shape[3] // BLOCK, BLOCK)
    result = jnp.einsum("szyxb,sbc->szyxc", blocks, block_inverse, precision=lax.Precision.HIGHEST)
    return result.reshape(shape)


def per_system(values):
    return values.reshape(values.shape[0], 1, 1, 1)


def on_device(right_side, labels, region_coeff, shift_index, shift_table, time_step, block_inverse):
    conductivity = cell_values(labels, region_coeff)
    cond_rim = padded_2(conductivity, (("gz", 0), ("gy", 1)), 1)
    padded_cond = jnp.pad(cond_rim, ((0, 0), (0, 0), (1, 1)))
    shift_values = jnp.sum(
        jnp.where(shift_index[:, None] == jnp.arange(shift_table.shape[0]), shift_table, 0.0),
        axis=1,
    )
    scale = time_step[0]
    residual = jnp.broadcast_to(right_side[None], (SHIFTS,) + right_side.shape)
    solution = jnp.zeros_like(residual)
    precond = precondition(residual, block_inverse)
    direction = precond
    rz_now = global_sum(jnp.sum(residual * precond, axis=(1, 2, 3)))
    for iteration in range(ITERS):
        padded = extend_field(direction)
        image = per_system(shift_values) * direction + scale * stencil(
            direction, padded, conductivity, padded_cond
        )
        curvature = global_sum(jnp.sum(direction * image, axis=(1, 2, 3)))
        alpha = per_system(rz_now / curvature)
        solution = solution + alpha * direction
        residual = residual - alpha * image
        precond = precondition(residual, block_inverse)
        rz_next = global_sum(jnp.sum(residual * precond, axis=(1, 2, 3)))
        direction = precond + per_system(rz_next / rz_now) * direction
        rz_now = rz_next
    return (solution, residual)


def solution(mesh):
    in_specs = (
        P(("sample", "gz"), "gy", None),
        P(("sample", "gz"), "gy", None),
        P("sample"),
        P("sample"),
        P(),
        P("sample"),
        P(),
    )
    out_specs = (P(None, ("sample", "gz"), "gy", None), P(None, ("sample", "gz"), "gy", None))
    return jax.shard_map(
        on_device, mesh=mesh, in_specs=in_specs, out_specs=out_specs, check_vma=False
    )
```

profile of v0, /device:TPU:0, one launch (start us, length us, event | category | flops | bytes accessed | tf_op | source)
XLA Modules:
  0.0 131.5 jit_solution(17609959154963669425)
XLA Ops:
  0.7 0.8 select_reduce_fusion
  1.5 0.1 copy.32
  1.6 1.3 collective-permute-start.1
  2.9 3.0 %collective-permute-start = (f32[1,16,256]{1,2,0:T(8,128)S(1)}, f32[1,16,256]{1,2,0:T(8,128)S(1)}, u32[]{:S(2)}, u32[]{:S(2)}) collective-permute-start(f32[1,16,256]{1,2,0:T(8,128)S(1)} %get-tuple-element.54), channel_id=1, source_target_pairs={{0,4},{4,8},{8,12},{1,5},{5,9},{9,13},{2,6},{6,10},{10,14},{3,7},{... | collective-permute-start | bytes 49160 | tf_op jit(solution)/shard_map/ppermute | solution.py:23
  6.0 0.9 copy_bitcast_fusion.1
  6.9 1.1 multiply_reduce_fusion.2
  8.0 1.0 copy-done.4
  9.0 1.3 collective-permute-start.5
  10.3 5.1 %collective-permute-start.4 = (f32[8,1,16,256]{3,2,1,0:T(8,128)S(1)}, f32[8,1,16,256]{3,2,1,0:T(8,128)S(1)}, u32[]{:S(2)}, u32[]{:S(2)}) collective-permute-start(f32[8,1,16,256]{3,2,1,0:T(8,128)S(1)} %get-tuple-element.19), channel_id=1, source_target_pairs={{0,4},{4,8},{8,12},{1,5},{5,9},{9,13},{2,6},{6,10},{10,14},{3,7},{... | collective-permute-start | bytes 393224 | tf_op jit(solution)/shard_map/ppermute | solution.py:23
  15.5 0.2 select_reduce_fusion.1
  16.4 0.1 copy.35
  16.5 0.1 copy.34
  16.6 3.5 %collective-permute-start.2 = (f32[10,1,256]{2,1,0:T(1,128)S(1)}, f32[10,1,256]{2,1,0:T(1,128)S(1)}, u32[]{:S(2)}, u32[]{:S(2)}) collective-permute-start(f32[10,1,256]{2,1,0:T(1,128)S(1)} %get-tuple-element.46), channel_id=1, source_target_pairs={{0,1},{1,2},{2,3},{4,5},{5,6},{6,7},{8,9},{9,10},{10,11},{12,13},{... | collective-permute-start | bytes 30728 | tf_op jit(solution)/shard_map/ppermute | solution.py:23
  20.1 1.3 collective-permute-start.3
  21.4 0.8 fusion.153
  22.1 3.5 %collective-permute-done.3 = f32[10,1,256]{2,1,0:T(1,128)S(1)} collective-permute-done((f32[10,1,256]{2,1,0:T(1,128)S(1)}, f32[10,1,256]{2,1,0:T(1,128)S(1)}, u32[]{:S(2)}, u32[]{:S(2)}) %collective-permute-start.3) | collective-permute-done | bytes 10272 | tf_op jit(solution)/shard_map/ppermute | solution.py:26
  25.6 0.2 select_maximum_fusion.6
  25.9 1.5 %fusion.157 = (f32[8,16,256]{2,1,0:T(8,128)S(1)}, f32[8,16,256]{2,1,0:T(8,128)S(1)}, f32[8,16,256]{2,1,0:T(8,128)S(1)}, f32[8,16,256]{2,1,0:T(8,128)S(1)}, f32[8...) fusion(f32[10,18,258]{2,1,0:T(8,128)S(1)} %select_maximum_fusio, ...), kind=kLoop, calls=%fused_computation.268 | loop fusion | flops 1179648 | bytes 4734976 | tf_op jit(solution)/shard_map/mul | solution.py:52
  27.5 0.1 constant_dynamic-update-slice_fusion.1
  27.6 0.1 fusion.160
  27.7 3.5 %collective-permute-start.6 = (f32[8,10,1,256]{3,2,1,0:T(1,128)S(1)}, f32[8,10,1,256]{3,2,1,0:T(1,128)S(1)}, u32[]{:S(2)}, u32[]{:S(2)}) collective-permute-start(f32[8,10,1,256]{3,2,1,0:T(1,128)S(1)} %get-tuple-element.14), channel_id=1, source_target_pairs={{0,1},{1,2},{2,3},{4,5},{5,6},{6,7},{8,9},{9,10},{10,11},{12,13},{... | collective-permute-start | bytes 245768 | tf_op jit(solution)/shard_map/ppermute | solution.py:23
  31.2 1.3 collective-permute-start.7
  32.5 0.9 fusion.156
  33.4 4.1 %collective-permute-done.7 = f32[8,10,1,256]{3,2,1,0:T(1,128)S(1)} collective-permute-done((f32[8,10,1,256]{3,2,1,0:T(1,128)S(1)}, f32[8,10,1,256]{3,2,1,0:T(1,128)S(1)}, u32[]{:S(2)}, u32[]{:S(2)}) %collective-permute-start.7) | collective-permute-done | bytes 81952 | tf_op jit(solution)/shard_map/ppermute | solution.py:26
  37.6 1.5 %select_maximum_fusion.4 = f32[8,10,18,258]{3,2,1,0:T(8,128)S(1)} fusion(f32[8,10,1,256]{3,2,1,0:T(1,128)S(1)} %collective-permute-done.7, f32[8,10,16,256]{3,2,1,0:T(8,128)S(1)} %constant_dynamic-update-slice_fusion, f32[8,10,1,256]{3,2,1,0:T(1,128)S(1)} %collective-permute-done.6), kind=kLoop, calls=%fused_computation.6 | loop fusion | flops 2972160 | bytes 2960640 | tf_op jit(solution)/shard_map/concatenate | solution.py:27
  39.1 9.8 %multiply_reduce_fusion.1 = (f32[8]{0:T(128)S(1)}, f32[8,8,16,256]{3,2,1,0:T(8,128)S(1)}) fusion(f32[8,8,16,256]{3,2,1,0:T(8,128)} %copy-done.4, f32[8,10,18,258]{3,2,1,0:T(8,128)S(1)} %select_maximum_fusion.4, f32[8,16,256]{2,1,0:T(8,128)} %get-tuple-element.37, f32[8,10,1,256]{3,2,1,0:T(1,128)} %copy-done.10, f32[8,10,16,256]{3,2,1,0:T(8,128)} %copy-done.3, ...), kind=kLoop, calls=%fused_computation.198 | loop fusion | flops 23592952 | bytes 27164740 | tf_op jit(solution)/shard_map/reduce_sum | solution.py:96
  49.0 9.9 %all-reduce.3 = (f32[8]{0:T(128)S(1)}, f32[8]{0:T(128)S(1)}) all-reduce(f32[8]{0:T(128)S(1)} %get-tuple-element.57, f32[8]{0:T(128)S(1)} %get-tuple-element.8), channel_id=1, replica_groups=mesh['sample'=2,'gz'=4,'gy'=4] {'gy'}, use_global_device_ids=true, to_apply=%region_1.2 | all-reduce | flops 16 | bytes 128 | tf_op jit(solution)/shard_map/psum | solution.py:62
  58.9 5.6 %all-reduce.4 = (f32[8]{0:T(128)S(1)}, f32[8]{0:T(128)S(1)}) all-reduce(f32[8]{0:T(128)S(1)} %get-tuple-element.2, f32[8]{0:T(128)S(1)} %get-tuple-element.3), channel_id=1, replica_groups=mesh['sample'=2,'gz'=4,'gy'=4] {'gz'}, use_global_device_ids=true, to_apply=%region_2.3 | all-reduce | flops 16 | bytes 128 | tf_op jit(solution)/shard_map/psum | solution.py:63
  64.6 1.2 convolution_bitcast_fusion
  65.8 1.0 copy-done.2
  66.7 0.3 fusion.40
  67.1 8.8 %psum.60 = f32[8]{0:T(128)S(1)} all-reduce(f32[8]{0:T(128)S(1)} %fusion.40), channel_id=1, replica_groups=mesh['sample'=2,'gz'=4,'gy'=4] {'gy'}, use_global_device_ids=true, to_apply=%region_9.10 | all-reduce | flops 8 | bytes 64 | tf_op jit(solution)/shard_map/psum | solution.py:62
  75.8 5.6 %psum.61 = f32[8]{0:T(128)S(1)} all-reduce(f32[8]{0:T(128)S(1)} %psum.60), channel_id=1, replica_groups=mesh['sample'=2,'gz'=4,'gy'=4] {'gz'}, use_global_device_ids=true, to_apply=%region_10.11 | all-reduce | flops 8 | bytes 64 | tf_op jit(solution)/shard_map/psum | solution.py:63
  81.5 1.5 %bitcast_add_fusion = f32[8,8,16,256]{3,2,1,0:T(8,128)S(1)} fusion(f32[8,8,2,2,8,128]{5,4,3,2,1,0:T(8,128)} %copy-done.2, f32[8]{0:T(128)S(1)} %div.10, f32[8,8,16,2,128]{4,2,3,1,0:T(8,128)S(1)} %get-tuple-element.58), kind=kLoop, calls=%fused_computation.59 | loop fusion | flops 524288 | bytes 3145760 | tf_op jit(solution)/shard_map/add | solution.py:102
  83.1 1.9 %collective-permute-start.8 = (f32[8,1,16,256]{3,2,1,0:T(8,128)S(1)}, f32[8,1,16,256]{3,2,1,0:T(8,128)S(1)}, u32[]{:S(2)}, u32[]{:S(2)}) collective-permute-start(f32[8,1,16,256]{3,2,1,0:T(8,128)S(1)} %get-tuple-element.16), channel_id=1, source_target_pairs={{0,4},{4,8},{8,12},{1,5},{5,9},{9,13},{2,6},{6,10},{10,14},{3,7},{... | collective-permute-start | bytes 393224 | tf_op jit(solution)/shard_map/ppermute | solution.py:23
  85.0 1.3 collective-permute-start.9
  86.3 3.4 %collective-permute-done.9 = f32[8,1,16,256]{3,2,1,0:T(8,128)S(1)} collective-permute-done((f32[8,1,16,256]{3,2,1,0:T(8,128)S(1)}, f32[8,1,16,256]{3,2,1,0:T(8,128)S(1)}, u32[]{:S(2)}, u32[]{:S(2)}) %collective-permute-start.9) | collective-permute-done | bytes 131104 | tf_op jit(solution)/shard_map/ppermute | solution.py:26
  89.7 0.1 pad_maximum_fusion.12
  89.8 3.5 %collective-permute-start.10 = (f32[8,10,1,256]{3,2,1,0:T(1,128)S(1)}, f32[8,10,1,256]{3,2,1,0:T(1,128)S(1)}, u32[]{:S(2)}, u32[]{:S(2)}) collective-permute-start(f32[8,10,1,256]{3,2,1,0:T(1,128)S(1)} %get-tuple-element.12), channel_id=1, source_target_pairs={{0,1},{1,2},{2,3},{4,5},{5,6},{6,7},{8,9},{9,10},{10,11},{12,13},{... | collective-permute-start | bytes 245768 | tf_op jit(solution)/shard_map/ppermute | solution.py:23
  93.3 1.5 %collective-permute-start.11 = (f32[8,10,1,256]{3,2,1,0:T(1,128)S(1)}, f32[8,10,1,256]{3,2,1,0:T(1,128)S(1)}, u32[]{:S(2)}, u32[]{:S(2)}) collective-permute-start(f32[8,10,1,256]{3,2,1,0:T(1,128)S(1)} %get-tuple-element.13), channel_id=1, source_target_pairs={{1,0},{2,1},{3,2},{5,4},{6,5},{7,6},{9,8},{10,9},{11,10},{13,12},{... | collective-permute-start | bytes 245768 | tf_op jit(solution)/shard_map/ppermute | solution.py:26
  94.8 0.6 collective-permute-done.10
  95.3 4.3 %collective-permute-done.11 = f32[8,10,1,256]{3,2,1,0:T(1,128)S(1)} collective-permute-done((f32[8,10,1,256]{3,2,1,0:T(1,128)S(1)}, f32[8,10,1,256]{3,2,1,0:T(1,128)S(1)}, u32[]{:S(2)}, u32[]{:S(2)}) %collective-permute-start.11) | collective-permute-done | bytes 81952 | tf_op jit(solution)/shard_map/ppermute | solution.py:26
  99.6 1.5 %select_maximum_fusion = f32[8,10,18,258]{3,2,1,0:T(8,128)S(1)} fusion(f32[8,10,1,256]{3,2,1,0:T(1,128)S(1)} %collective-permute-done.11, f32[8,10,1,256]{3,2,1,0:T(1,128)S(1)} %collective-permute-done.10, f32[8,1,16,256]{3,2,1,0:T(8,128)S(1)} %collective-permute-done.9, f32[8,8,16,256]{3,2,1,0:T(8,128)S(1)} %bitcast_add_fusion, ...), kind=kLoop, calls=%fused_computation.2 | loop fusion | flops 4458240 | bytes 2960640 | tf_op jit(solution)/shard_map/concatenate | solution.py:27
  101.1 2.4 %maximum_maximum_fusion = (f32[8,10,17,256]{3,2,1,0:T(8,128)}, f32[8,10,17,256]{3,2,1,0:T(8,128)}) fusion(f32[8,1,16,256]{3,2,1,0:T(8,128)S(1)} %collective-permute-done.9, f32[8,8,16,256]{3,2,1,0:T(8,128)S(1)} %bitcast_add_fusion, f32[8,1,16,256]{3,2,1,0:T(8,128)S(1)} %collective-permute-done.8, f32[8,10,1,256]{3,2,1,0:T(1,128)S(1)} %collective-permute-done.10, ...), kind=kLoop, calls=%fused_computation.17 | loop fusion | flops 2088960 | bytes 4259840 | tf_op jit(solution)/shard_map/concatenate | solution.py:27
  103.5 9.4 %multiply_reduce_fusion = (f32[8]{0:T(128)S(1)}, f32[8,8,16,256]{3,2,1,0:T(8,128)}) fusion(f32[8,8,16,256]{3,2,1,0:T(8,128)S(1)} %bitcast_add_fusion, f32[8,10,18,258]{3,2,1,0:T(8,128)S(1)} %select_maximum_fusion, f32[8,16,256]{2,1,0:T(8,128)} %get-tuple-element.37, f32[8,10,17,256]{3,2,1,0:T(8,128)} %get-tuple-element.11, ...), kind=kLoop, calls=%fused_computation.196 | loop fusion | flops 22020088 | bytes 30933060 | tf_op jit(solution)/shard_map/reduce_sum | solution.py:96
  112.9 8.4 %psum.62 = f32[8]{0:T(128)S(1)} all-reduce(f32[8]{0:T(128)S(1)} %get-tuple-element.6), channel_id=1, replica_groups=mesh['sample'=2,'gz'=4,'gy'=4] {'gy'}, use_global_device_ids=true, to_apply=%region_12.13 | all-reduce | flops 8 | bytes 64 | tf_op jit(solution)/shard_map/psum | solution.py:62
  121.3 6.8 %psum.63 = f32[8]{0:T(128)S(1)} all-reduce(f32[8]{0:T(128)S(1)} %psum.62), channel_id=1, replica_groups=mesh['sample'=2,'gz'=4,'gy'=4] {'gz'}, use_global_device_ids=true, to_apply=%region_13.14 | all-reduce | flops 8 | bytes 64 | tf_op jit(solution)/shard_map/psum | solution.py:63
  128.1 3.4 %multiply_subtract_fusion = (f32[8,8,16,256]{3,2,1,0:T(8,128)}, f32[8,8,16,256]{3,2,1,0:T(8,128)}) fusion(f32[8,8,16,256]{3,2,1,0:T(8,128)} %get-tuple-element.7, f32[8,8,16,256]{3,2,1,0:T(8,128)} %copy-done.1, f32[8]{0:T(128)S(1)} %div.11, f32[8,16,256]{2,1,0:T(8,128)S(1)} %copy-done.5, f32[8]{0:T(128)S(1)} %div.9, ...), kind=kLoop, calls=%fused_computation.194 | loop fusion | flops 1835008 | bytes 6422592 | tf_op jit(solution)/shard_map/sub | solution.py:99
  (45 shorter events, 0.4 us)
Async XLA Ops:
  0.6 6.2 %copy-start = (f32[8,128,128]{2,1,0:T(8,128)S(1)}, f32[8,128,128]{2,1,0:T(8,128)}, u32[]{:S(2)}) copy-start(f32[8,128,128]{2,1,0:T(8,128)} %param.13) | copy-start | bytes 1572868
  0.6 14.8 %copy-start.11 = (f32[16]{0:T(128)S(1)}, f32[16]{0:T(128)}, u32[]{:S(2)}) copy-start(f32[16]{0:T(128)} %param.11) | copy-start | bytes 196
  0.7 14.8 %copy-start.12 = (s32[8]{0:T(128)S(1)}, s32[8]{0:T(128)}, u32[]{:S(2)}) copy-start(s32[8]{0:T(128)} %param.10) | copy-start | bytes 100
  1.6 14.8 %collective-permute-start.1 = (f32[1,16,256]{1,2,0:T(8,128)S(1)}, f32[1,16,256]{1,2,0:T(8,128)S(1)}, u32[]{:S(2)}, u32[]{:S(2)}) collective-permute-start(f32[1,16,256]{1,2,0:T(8,128)S(1)} %get-tuple-element.54), channel_id=1, source_target_pairs={{4,0},{8,4},{12,8},{5,1},{9,5},{13,9},{6,2},{10,6},{14,10},{7,3},{... | collective-permute-start | bytes 49160 | tf_op jit(solution)/shard_map/ppermute | solution.py:26
  2.9 13.6 %collective-permute-start = (f32[1,16,256]{1,2,0:T(8,128)S(1)}, f32[1,16,256]{1,2,0:T(8,128)S(1)}, u32[]{:S(2)}, u32[]{:S(2)}) collective-permute-start(f32[1,16,256]{1,2,0:T(8,128)S(1)} %get-tuple-element.54), channel_id=1, source_target_pairs={{0,4},{4,8},{8,12},{1,5},{5,9},{9,13},{2,6},{6,10},{10,14},{3,7},{... | collective-permute-start | bytes 49160 | tf_op jit(solution)/shard_map/ppermute | solution.py:23
  8.0 1.0 copy-start.4
  9.0 18.5 %collective-permute-start.5 = (f32[8,1,16,256]{3,2,1,0:T(8,128)S(1)}, f32[8,1,16,256]{3,2,1,0:T(8,128)S(1)}, u32[]{:S(2)}, u32[]{:S(2)}) collective-permute-start(f32[8,1,16,256]{3,2,1,0:T(8,128)S(1)} %get-tuple-element.18), channel_id=1, source_target_pairs={{4,0},{8,4},{12,8},{5,1},{9,5},{13,9},{6,2},{10,6},{14,10},{7,3},{... | collective-permute-start | bytes 393224 | tf_op jit(solution)/shard_map/ppermute | solution.py:26
  10.3 17.1 %collective-permute-start.4 = (f32[8,1,16,256]{3,2,1,0:T(8,128)S(1)}, f32[8,1,16,256]{3,2,1,0:T(8,128)S(1)}, u32[]{:S(2)}, u32[]{:S(2)}) collective-permute-start(f32[8,1,16,256]{3,2,1,0:T(8,128)S(1)} %get-tuple-element.19), channel_id=1, source_target_pairs={{0,4},{4,8},{8,12},{1,5},{5,9},{9,13},{2,6},{6,10},{10,14},{3,7},{... | collective-permute-start | bytes 393224 | tf_op jit(solution)/shard_map/ppermute | solution.py:23
  16.6 5.5 %collective-permute-start.2 = (f32[10,1,256]{2,1,0:T(1,128)S(1)}, f32[10,1,256]{2,1,0:T(1,128)S(1)}, u32[]{:S(2)}, u32[]{:S(2)}) collective-permute-start(f32[10,1,256]{2,1,0:T(1,128)S(1)} %get-tuple-element.46), channel_id=1, source_target_pairs={{0,1},{1,2},{2,3},{4,5},{5,6},{6,7},{8,9},{9,10},{10,11},{12,13},{... | collective-permute-start | bytes 30728 | tf_op jit(solution)/shard_map/ppermute | solution.py:23
  20.1 5.6 %collective-permute-start.3 = (f32[10,1,256]{2,1,0:T(1,128)S(1)}, f32[10,1,256]{2,1,0:T(1,128)S(1)}, u32[]{:S(2)}, u32[]{:S(2)}) collective-permute-start(f32[10,1,256]{2,1,0:T(1,128)S(1)} %get-tuple-element.47), channel_id=1, source_target_pairs={{1,0},{2,1},{3,2},{5,4},{6,5},{7,6},{9,8},{10,9},{11,10},{13,12},{... | collective-permute-start | bytes 30728 | tf_op jit(solution)/shard_map/ppermute | solution.py:26
  27.4 11.7 %copy-start.6 = (f32[8,16,256]{2,1,0:T(8,128)}, f32[8,16,256]{2,1,0:T(8,128)S(1)}, u32[]{:S(2)}) copy-start(f32[8,16,256]{2,1,0:T(8,128)S(1)} %get-tuple-element.25) | copy-start | bytes 393220
  27.4 11.7 %copy-start.7 = (f32[8,16,256]{2,1,0:T(8,128)}, f32[8,16,256]{2,1,0:T(8,128)S(1)}, u32[]{:S(2)}) copy-start(f32[8,16,256]{2,1,0:T(8,128)S(1)} %get-tuple-element.26) | copy-start | bytes 393220
  27.4 11.6 %copy-start.9 = (f32[8,1,16,256]{3,2,1,0:T(8,128)}, f32[8,1,16,256]{3,2,1,0:T(8,128)S(1)}, u32[]{:S(2)}) copy-start(f32[8,1,16,256]{3,2,1,0:T(8,128)S(1)} %collective-permute-done.4) | copy-start | bytes 393220
  27.6 11.5 %copy-start.8 = (f32[8,1,16,256]{3,2,1,0:T(8,128)}, f32[8,1,16,256]{3,2,1,0:T(8,128)S(1)}, u32[]{:S(2)}) copy-start(f32[8,1,16,256]{3,2,1,0:T(8,128)S(1)} %collective-permute-done.5) | copy-start | bytes 393220
  27.6 11.5 %copy-start.3 = (f32[8,10,16,256]{3,2,1,0:T(8,128)}, f32[8,10,16,256]{3,2,1,0:T(8,128)S(1)}, u32[]{:S(2)}) copy-start(f32[8,10,16,256]{3,2,1,0:T(8,128)S(1)} %constant_dynamic-update-slice_fusion) | copy-start | bytes 3932164
  27.7 5.7 %collective-permute-start.6 = (f32[8,10,1,256]{3,2,1,0:T(1,128)S(1)}, f32[8,10,1,256]{3,2,1,0:T(1,128)S(1)}, u32[]{:S(2)}, u32[]{:S(2)}) collective-permute-start(f32[8,10,1,256]{3,2,1,0:T(1,128)S(1)} %get-tuple-element.14), channel_id=1, source_target_pairs={{0,1},{1,2},{2,3},{4,5},{5,6},{6,7},{8,9},{9,10},{10,11},{12,13},{... | collective-permute-start | bytes 245768 | tf_op jit(solution)/shard_map/ppermute | solution.py:23
  31.2 6.3 %collective-permute-start.7 = (f32[8,10,1,256]{3,2,1,0:T(1,128)S(1)}, f32[8,10,1,256]{3,2,1,0:T(1,128)S(1)}, u32[]{:S(2)}, u32[]{:S(2)}) collective-permute-start(f32[8,10,1,256]{3,2,1,0:T(1,128)S(1)} %get-tuple-element.15), channel_id=1, source_target_pairs={{1,0},{2,1},{3,2},{5,4},{6,5},{7,6},{9,8},{10,9},{11,10},{13,12},{... | collective-permute-start | bytes 245768 | tf_op jit(solution)/shard_map/ppermute | solution.py:26
  37.6 1.5 %copy-start.10 = (f32[8,10,1,256]{3,2,1,0:T(1,128)}, f32[8,10,1,256]{3,2,1,0:T(1,128)S(1)}, u32[]{:S(2)}) copy-start(f32[8,10,1,256]{3,2,1,0:T(1,128)S(1)} %collective-permute-done.7) | copy-start | bytes 245764
  39.1 25.4 %copy-start.5 = (f32[8,16,256]{2,1,0:T(8,128)S(1)}, f32[8,16,256]{2,1,0:T(8,128)}, u32[]{:S(2)}) copy-start(f32[8,16,256]{2,1,0:T(8,128)} %param.7) | copy-start | bytes 393220
  49.0 32.5 %copy-start.1 = (f32[8,8,16,256]{3,2,1,0:T(8,128)}, f32[8,8,16,256]{3,2,1,0:T(8,128)S(1)}, u32[]{:S(2)}) copy-start(f32[8,8,16,256]{3,2,1,0:T(8,128)S(1)} %get-tuple-element.9) | copy-start | bytes 3145732
  65.8 1.0 copy-start.2
  83.1 3.2 %collective-permute-start.8 = (f32[8,1,16,256]{3,2,1,0:T(8,128)S(1)}, f32[8,1,16,256]{3,2,1,0:T(8,128)S(1)}, u32[]{:S(2)}, u32[]{:S(2)}) collective-permute-start(f32[8,1,16,256]{3,2,1,0:T(8,128)S(1)} %get-tuple-element.16), channel_id=1, source_target_pairs={{0,4},{4,8},{8,12},{1,5},{5,9},{9,13},{2,6},{6,10},{10,14},{3,7},{... | collective-permute-start | bytes 393224 | tf_op jit(solution)/shard_map/ppermute | solution.py:23
  85.0 4.7 %collective-permute-start.9 = (f32[8,1,16,256]{3,2,1,0:T(8,128)S(1)}, f32[8,1,16,256]{3,2,1,0:T(8,128)S(1)}, u32[]{:S(2)}, u32[]{:S(2)}) collective-permute-start(f32[8,1,16,256]{3,2,1,0:T(8,128)S(1)} %get-tuple-element.17), channel_id=1, source_target_pairs={{4,0},{8,4},{12,8},{5,1},{9,5},{13,9},{6,2},{10,6},{14,10},{7,3},{... | collective-permute-start | bytes 393224 | tf_op jit(solution)/shard_map/ppermute | solution.py:26
  89.8 5.5 %collective-permute-start.10 = (f32[8,10,1,256]{3,2,1,0:T(1,128)S(1)}, f32[8,10,1,256]{3,2,1,0:T(1,128)S(1)}, u32[]{:S(2)}, u32[]{:S(2)}) collective-permute-start(f32[8,10,1,256]{3,2,1,0:T(1,128)S(1)} %get-tuple-element.12), channel_id=1, source_target_pairs={{0,1},{1,2},{2,3},{4,5},{5,6},{6,7},{8,9},{9,10},{10,11},{12,13},{... | collective-permute-start | bytes 245768 | tf_op jit(solution)/shard_map/ppermute | solution.py:23
  93.3 6.3 %collective-permute-start.11 = (f32[8,10,1,256]{3,2,1,0:T(1,128)S(1)}, f32[8,10,1,256]{3,2,1,0:T(1,128)S(1)}, u32[]{:S(2)}, u32[]{:S(2)}) collective-permute-start(f32[8,10,1,256]{3,2,1,0:T(1,128)S(1)} %get-tuple-element.13), channel_id=1, source_target_pairs={{1,0},{2,1},{3,2},{5,4},{6,5},{7,6},{9,8},{10,9},{11,10},{13,12},{... | collective-permute-start | bytes 245768 | tf_op jit(solution)/shard_map/ppermute | solution.py:26
where the time goes:
time: 132 us
  blocking collectives  45.2 us (34%)
  other arithmetic  34.4 us (26%)
  starting transfers between devices  28.4 us (22%)
  waiting for transfers between devices  15.9 us (12%)
  local copies, waits for them, and re-layouts  3.56 us (3%)
  matrix products  2.26 us (2%)
  between operations  1.71 us (1%)
    psum x3, blocking collectives, global_sum(): row_sum = lax.psum(values, 'gy')  27.1 us
    ppermute x6, starting transfers between devices, padded_2(): lax.ppermute(lax.slice_in_dim(block, block.shape[dim] - width, None, axis...  20.5 us
    reduce_sum x2, other arithmetic, on_device(): curvature = global_sum(jnp.sum(direction * image, axis=(1, 2, 3)))  19.2 us
    psum x3, blocking collectives, global_sum(): return lax.psum(row_sum, 'gz')  18.1 us
    ppermute x6, waiting for transfers between devices, padded_2(): lax.ppermute(lax.slice_in_dim(block, 0, width, axis=dim), axis, backward)  15.4 us
    ppermute x6, starting transfers between devices, padded_2(): lax.ppermute(lax.slice_in_dim(block, 0, width, axis=dim), axis, backward)  7.93 us
    concatenate x5, other arithmetic, padded_2(): block = jnp.concatenate([low, block, high], axis=dim)  5.62 us
    sub x1, other arithmetic, on_device(): residual = residual - alpha * image  3.39 us
  transfers between devices with their start and end apart: 12, of which 5 were waited for; matrix products, arithmetic and copies ran while one was open for 5% of the time, Pallas kernels for 0%

commit v1 on v0

--- a/solution.py
+++ b/solution.py
@@ -59,7 +59,7 @@
 
 
 def global_sum(values):
-    row_sum = lax.psum(values, "gy")
+    row_sum = jnp.sum(lax.all_gather(values, "gy"), axis=0)
     return lax.psum(row_sum, "gz")
 
 

time: 132 us -> 136 us (1.030)
  local copies, waits for them, and re-layouts: 3.56 us -> 5.44 us
  blocking collectives: 45.2 us -> 46.6 us
    psum x3 -> x0, blocking collectives: 27.1 us -> none  [global_sum(): row_sum = lax.psum(values, 'gy')]
    unnamed x0 -> x3, blocking collectives: none -> 27 us
    unnamed x28 -> x39, local copies, waits for them, and re-layouts: 2.09 us -> 3.64 us
    psum x3, blocking collectives: 18.1 us -> 19.6 us  [global_sum(): return lax.psum(row_sum, 'gz')]
  transfers between devices with their start and end apart: 12 -> 12, of which waited for: 5 -> 6; matrix products, arithmetic and copies ran while one was open for 5% -> 5% of each run, Pallas kernels for 0% -> 0%
where the time goes in v1:
time: 136 us
  blocking collectives  46.6 us (34%)
  other arithmetic  34.3 us (25%)
  starting transfers between devices  28.2 us (21%)
  waiting for transfers between devices  16.5 us (12%)
  local copies, waits for them, and re-layouts  5.44 us (4%)
  between operations  2.43 us (2%)
  matrix products  2.26 us (2%)
    unnamed x3, blocking collectives  27 us
    ppermute x6, starting transfers between devices, padded_2(): lax.ppermute(lax.slice_in_dim(block, block.shape[dim] - width, None, axis...  20.2 us
    psum x3, blocking collectives, global_sum(): return lax.psum(row_sum, 'gz')  19.6 us
    reduce_sum x2, other arithmetic, on_device(): curvature = global_sum(jnp.sum(direction * image, axis=(1, 2, 3)))  19.1 us
    ppermute x6, waiting for transfers between devices, padded_2(): lax.ppermute(lax.slice_in_dim(block, 0, width, axis=dim), axis, backward)  15.3 us
    ppermute x6, starting transfers between devices, padded_2(): lax.ppermute(lax.slice_in_dim(block, 0, width, axis=dim), axis, backward)  7.93 us
    concatenate x5, other arithmetic, padded_2(): block = jnp.concatenate([low, block, high], axis=dim)  5.6 us
    unnamed x39, local copies, waits for them, and re-layouts  3.64 us
  transfers between devices with their start and end apart: 12, of which 6 were waited for; matrix products, arithmetic and copies ran while one was open for 5% of the time, Pallas kernels for 0%

profile of v1, /device:TPU:0, one launch (start us, length us, event | category | flops | bytes accessed | tf_op | source)
XLA Modules:
  0.0 135.7 jit_solution(16838504016877632698)
XLA Ops:
  0.7 0.8 select_reduce_fusion
  1.6 2.4 %collective-permute-start = (f32[1,16,256]{1,2,0:T(8,128)S(1)}, f32[1,16,256]{1,2,0:T(8,128)S(1)}, u32[]{:S(2)}, u32[]{:S(2)}) collective-permute-start(f32[1,16,256]{1,2,0:T(8,128)S(1)} %get-tuple-element.54), channel_id=1, source_target_pairs={{0,4},{4,8},{8,12},{1,5},{5,9},{9,13},{2,6},{6,10},{10,14},{3,7},{... | collective-permute-start | bytes 49160 | tf_op jit(solution)/shard_map/ppermute | solution.py:23
  4.0 1.3 collective-permute-start.1
  5.3 0.9 copy_bitcast_fusion.1
  6.3 1.1 multiply_reduce_fusion.2
  7.4 1.0 copy-done.4
  8.4 5.1 %collective-permute-start.4 = (f32[8,1,16,256]{3,2,1,0:T(8,128)S(1)}, f32[8,1,16,256]{3,2,1,0:T(8,128)S(1)}, u32[]{:S(2)}, u32[]{:S(2)}) collective-permute-start(f32[8,1,16,256]{3,2,1,0:T(8,128)S(1)} %get-tuple-element.19), channel_id=1, source_target_pairs={{0,4},{4,8},{8,12},{1,5},{5,9},{9,13},{2,6},{6,10},{10,14},{3,7},{... | collective-permute-start | bytes 393224 | tf_op jit(solution)/shard_map/ppermute | solution.py:23
  13.6 1.3 collective-permute-start.5
  14.9 0.2 select_reduce_fusion.1
  15.8 0.6 dynamic-slice
  17.1 0.2 dynamic-update-slice
  17.5 3.5 %collective-permute-start.2 = (f32[10,1,256]{2,1,0:T(1,128)S(1)}, f32[10,1,256]{2,1,0:T(1,128)S(1)}, u32[]{:S(2)}, u32[]{:S(2)}) collective-permute-start(f32[10,1,256]{2,1,0:T(1,128)S(1)} %get-tuple-element.46), channel_id=1, source_target_pairs={{0,1},{1,2},{2,3},{4,5},{5,6},{6,7},{8,9},{9,10},{10,11},{12,13},{... | collective-permute-start | bytes 30728 | tf_op jit(solution)/shard_map/ppermute | solution.py:23
  21.0 1.3 collective-permute-start.3
  22.3 0.7 fusion.153
  23.0 3.5 %collective-permute-done.3 = f32[10,1,256]{2,1,0:T(1,128)S(1)} collective-permute-done((f32[10,1,256]{2,1,0:T(1,128)S(1)}, f32[10,1,256]{2,1,0:T(1,128)S(1)}, u32[]{:S(2)}, u32[]{:S(2)}) %collective-permute-start.3) | collective-permute-done | bytes 10272 | tf_op jit(solution)/shard_map/ppermute | solution.py:26
  26.5 0.2 select_maximum_fusion.6
  26.8 1.5 %fusion.157 = (f32[8,16,256]{2,1,0:T(8,128)S(1)}, f32[8,16,256]{2,1,0:T(8,128)S(1)}, f32[8,16,256]{2,1,0:T(8,128)S(1)}, f32[8,16,256]{2,1,0:T(8,128)S(1)}, f32[8...) fusion(f32[10,18,258]{2,1,0:T(8,128)S(1)} %select_maximum_fusio, ...), kind=kLoop, calls=%fused_computation.268 | loop fusion | flops 1179648 | bytes 4734976 | tf_op jit(solution)/shard_map/mul | solution.py:52
  28.6 3.5 %collective-permute-start.6 = (f32[8,10,1,256]{3,2,1,0:T(1,128)S(1)}, f32[8,10,1,256]{3,2,1,0:T(1,128)S(1)}, u32[]{:S(2)}, u32[]{:S(2)}) collective-permute-start(f32[8,10,1,256]{3,2,1,0:T(1,128)S(1)} %get-tuple-element.14), channel_id=1, source_target_pairs={{0,1},{1,2},{2,3},{4,5},{5,6},{6,7},{8,9},{9,10},{10,11},{12,13},{... | collective-permute-start | bytes 245768 | tf_op jit(solution)/shard_map/ppermute | solution.py:23
  32.1 1.3 collective-permute-start.7
  33.4 0.9 fusion.156
  34.4 0.6 collective-permute-done.6
  34.9 4.1 %collective-permute-done.7 = f32[8,10,1,256]{3,2,1,0:T(1,128)S(1)} collective-permute-done((f32[8,10,1,256]{3,2,1,0:T(1,128)S(1)}, f32[8,10,1,256]{3,2,1,0:T(1,128)S(1)}, u32[]{:S(2)}, u32[]{:S(2)}) %collective-permute-start.7) | collective-permute-done | bytes 81952 | tf_op jit(solution)/shard_map/ppermute | solution.py:26
  39.0 1.5 %select_maximum_fusion.4 = f32[8,10,18,258]{3,2,1,0:T(8,128)S(1)} fusion(f32[8,10,1,256]{3,2,1,0:T(1,128)S(1)} %collective-permute-done.7, f32[8,10,16,256]{3,2,1,0:T(8,128)S(1)} %constant_dynamic-update-slice_fusion, f32[8,10,1,256]{3,2,1,0:T(1,128)S(1)} %collective-permute-done.6), kind=kLoop, calls=%fused_computation.6 | loop fusion | flops 2972160 | bytes 2960640 | tf_op jit(solution)/shard_map/concatenate | solution.py:27
  40.6 9.7 %multiply_reduce_fusion.1 = (f32[8]{0:T(128)S(1)}, f32[8,8,16,256]{3,2,1,0:T(8,128)S(1)}) fusion(f32[8,8,16,256]{3,2,1,0:T(8,128)} %copy-done.4, f32[8,10,18,258]{3,2,1,0:T(8,128)S(1)} %select_maximum_fusion.4, f32[8,16,256]{2,1,0:T(8,128)} %get-tuple-element.37, f32[8,10,1,256]{3,2,1,0:T(1,128)} %copy-done.10, f32[8,10,16,256]{3,2,1,0:T(8,128)} %copy-done.3, ...), kind=kLoop, calls=%fused_computation.198 | loop fusion | flops 23592952 | bytes 27164740 | tf_op jit(solution)/shard_map/reduce_sum | solution.py:96
  50.3 0.2 dynamic-update-slice.1
  50.5 9.9 %all-reduce.7 = (f32[32]{0:T(128)S(1)}, f32[32]{0:T(128)S(1)}) all-reduce(f32[32]{0:T(128)S(1)} %dynamic-update-slice, f32[32]{0:T(128)S(1)} %dynamic-update-slice.1), channel_id=2, replica_groups=mesh['sample'=2,'gz'=4,'gy'=4] {'gy'}, use_global_device_ids=true, to_apply=%add.3 | all-reduce | flops 64 | bytes 512
  60.7 7.0 %all-reduce.8 = (f32[8]{0:T(128)S(1)}, f32[8]{0:T(128)S(1)}) all-reduce(f32[8]{0:T(128)S(1)} %reduce_sum.91, f32[8]{0:T(128)S(1)} %reduce_sum.95), channel_id=1, replica_groups=mesh['sample'=2,'gz'=4,'gy'=4] {'gz'}, use_global_device_ids=true, to_apply=%region_2.3 | all-reduce | flops 16 | bytes 128 | tf_op jit(solution)/shard_map/psum | solution.py:63
  67.7 1.2 convolution_bitcast_fusion
  68.9 1.0 copy-done.2
  69.8 0.3 fusion.40
  70.1 0.2 dynamic-update-slice.2
  70.4 8.8 %all-reduce.5 = f32[32]{0:T(128)S(1)} all-reduce(f32[32]{0:T(128)S(1)} %dynamic-update-slice.2), channel_id=4, replica_groups=mesh['sample'=2,'gz'=4,'gy'=4] {'gy'}, use_global_device_ids=true, to_apply=%add.5 | all-reduce | flops 32 | bytes 256
  79.3 5.8 %psum.30 = f32[8]{0:T(128)S(1)} all-reduce(f32[8]{0:T(128)S(1)} %reduce_sum.97), channel_id=1, replica_groups=mesh['sample'=2,'gz'=4,'gy'=4] {'gz'}, use_global_device_ids=true, to_apply=%region_10.11 | all-reduce | flops 8 | bytes 64 | tf_op jit(solution)/shard_map/psum | solution.py:63
  85.0 1.5 %bitcast_add_fusion = f32[8,8,16,256]{3,2,1,0:T(8,128)S(1)} fusion(f32[8,8,2,2,8,128]{5,4,3,2,1,0:T(8,128)} %copy-done.2, f32[8]{0:T(128)S(1)} %div.10, f32[8,8,16,2,128]{4,2,3,1,0:T(8,128)S(1)} %get-tuple-element.58), kind=kLoop, calls=%fused_computation.59 | loop fusion | flops 524288 | bytes 3145760 | tf_op jit(solution)/shard_map/add | solution.py:102
  86.6 2.3 %collective-permute-start.8 = (f32[8,1,16,256]{3,2,1,0:T(8,128)S(1)}, f32[8,1,16,256]{3,2,1,0:T(8,128)S(1)}, u32[]{:S(2)}, u32[]{:S(2)}) collective-permute-start(f32[8,1,16,256]{3,2,1,0:T(8,128)S(1)} %get-tuple-element.16), channel_id=1, source_target_pairs={{0,4},{4,8},{8,12},{1,5},{5,9},{9,13},{2,6},{6,10},{10,14},{3,7},{... | collective-permute-start | bytes 393224 | tf_op jit(solution)/shard_map/ppermute | solution.py:23
  88.9 1.3 collective-permute-start.9
  90.2 3.4 %collective-permute-done.9 = f32[8,1,16,256]{3,2,1,0:T(8,128)S(1)} collective-permute-done((f32[8,1,16,256]{3,2,1,0:T(8,128)S(1)}, f32[8,1,16,256]{3,2,1,0:T(8,128)S(1)}, u32[]{:S(2)}, u32[]{:S(2)}) %collective-permute-start.9) | collective-permute-done | bytes 131104 | tf_op jit(solution)/shard_map/ppermute | solution.py:26
  93.7 3.5 %collective-permute-start.10 = (f32[8,10,1,256]{3,2,1,0:T(1,128)S(1)}, f32[8,10,1,256]{3,2,1,0:T(1,128)S(1)}, u32[]{:S(2)}, u32[]{:S(2)}) collective-permute-start(f32[8,10,1,256]{3,2,1,0:T(1,128)S(1)} %get-tuple-element.12), channel_id=1, source_target_pairs={{0,1},{1,2},{2,3},{4,5},{5,6},{6,7},{8,9},{9,10},{10,11},{12,13},{... | collective-permute-start | bytes 245768 | tf_op jit(solution)/shard_map/ppermute | solution.py:23
  97.2 1.5 %collective-permute-start.11 = (f32[8,10,1,256]{3,2,1,0:T(1,128)S(1)}, f32[8,10,1,256]{3,2,1,0:T(1,128)S(1)}, u32[]{:S(2)}, u32[]{:S(2)}) collective-permute-start(f32[8,10,1,256]{3,2,1,0:T(1,128)S(1)} %get-tuple-element.13), channel_id=1, source_target_pairs={{1,0},{2,1},{3,2},{5,4},{6,5},{7,6},{9,8},{10,9},{11,10},{13,12},{... | collective-permute-start | bytes 245768 | tf_op jit(solution)/shard_map/ppermute | solution.py:26
  98.7 0.6 collective-permute-done.10
  99.2 4.3 %collective-permute-done.11 = f32[8,10,1,256]{3,2,1,0:T(1,128)S(1)} collective-permute-done((f32[8,10,1,256]{3,2,1,0:T(1,128)S(1)}, f32[8,10,1,256]{3,2,1,0:T(1,128)S(1)}, u32[]{:S(2)}, u32[]{:S(2)}) %collective-permute-start.11) | collective-permute-done | bytes 81952 | tf_op jit(solution)/shard_map/ppermute | solution.py:26
  103.5 2.3 %maximum_maximum_fusion = (f32[8,10,17,256]{3,2,1,0:T(8,128)}, f32[8,10,17,256]{3,2,1,0:T(8,128)}) fusion(f32[8,1,16,256]{3,2,1,0:T(8,128)S(1)} %collective-permute-done.9, f32[8,8,16,256]{3,2,1,0:T(8,128)S(1)} %bitcast_add_fusion, f32[8,1,16,256]{3,2,1,0:T(8,128)S(1)} %collective-permute-done.8, f32[8,10,1,256]{3,2,1,0:T(1,128)S(1)} %collective-permute-done.10, ...), kind=kLoop, calls=%fused_computation.17 | loop fusion | flops 2088960 | bytes 4259840 | tf_op jit(solution)/shard_map/concatenate | solution.py:27
  105.9 1.5 %select_maximum_fusion = f32[8,10,18,258]{3,2,1,0:T(8,128)S(1)} fusion(f32[8,10,1,256]{3,2,1,0:T(1,128)S(1)} %collective-permute-done.11, f32[8,10,1,256]{3,2,1,0:T(1,128)S(1)} %collective-permute-done.10, f32[8,1,16,256]{3,2,1,0:T(8,128)S(1)} %collective-permute-done.9, f32[8,8,16,256]{3,2,1,0:T(8,128)S(1)} %bitcast_add_fusion, ...), kind=kLoop, calls=%fused_computation.2 | loop fusion | flops 4458240 | bytes 2960640 | tf_op jit(solution)/shard_map/concatenate | solution.py:27
  107.4 9.4 %multiply_reduce_fusion = (f32[8]{0:T(128)S(1)}, f32[8,8,16,256]{3,2,1,0:T(8,128)}) fusion(f32[8,8,16,256]{3,2,1,0:T(8,128)S(1)} %bitcast_add_fusion, f32[8,10,18,258]{3,2,1,0:T(8,128)S(1)} %select_maximum_fusion, f32[8,16,256]{2,1,0:T(8,128)} %get-tuple-element.37, f32[8,10,17,256]{3,2,1,0:T(8,128)} %get-tuple-element.11, ...), kind=kLoop, calls=%fused_computation.196 | loop fusion | flops 22020088 | bytes 30933060 | tf_op jit(solution)/shard_map/reduce_sum | solution.py:96
  116.8 0.2 dynamic-update-slice.3
  117.0 8.3 %all-reduce.6 = f32[32]{0:T(128)S(1)} all-reduce(f32[32]{0:T(128)S(1)} %dynamic-update-slice.3), channel_id=5, replica_groups=mesh['sample'=2,'gz'=4,'gy'=4] {'gy'}, use_global_device_ids=true, to_apply=%add.6 | all-reduce | flops 32 | bytes 256
  125.5 6.9 %psum.31 = f32[8]{0:T(128)S(1)} all-reduce(f32[8]{0:T(128)S(1)} %reduce_sum.99), channel_id=1, replica_groups=mesh['sample'=2,'gz'=4,'gy'=4] {'gz'}, use_global_device_ids=true, to_apply=%region_13.14 | all-reduce | flops 8 | bytes 64 | tf_op jit(solution)/shard_map/psum | solution.py:63
  132.3 3.4 %multiply_subtract_fusion = (f32[8,8,16,256]{3,2,1,0:T(8,128)}, f32[8,8,16,256]{3,2,1,0:T(8,128)}) fusion(f32[8,8,16,256]{3,2,1,0:T(8,128)} %get-tuple-element.7, f32[8,8,16,256]{3,2,1,0:T(8,128)} %copy-done.1, f32[8]{0:T(128)S(1)} %div.11, f32[8,16,256]{2,1,0:T(8,128)S(1)} %copy-done.5, f32[8]{0:T(128)S(1)} %div.9, ...), kind=kLoop, calls=%fused_computation.194 | loop fusion | flops 1835008 | bytes 6422592 | tf_op jit(solution)/shard_map/sub | solution.py:99
  (64 shorter events, 1.4 us)
Async XLA Ops:
  0.6 5.6 %copy-start = (f32[8,128,128]{2,1,0:T(8,128)S(1)}, f32[8,128,128]{2,1,0:T(8,128)}, u32[]{:S(2)}) copy-start(f32[8,128,128]{2,1,0:T(8,128)} %param.13) | copy-start | bytes 1572868
  0.6 15.2 %copy-start.13 = (u32[32]{0:T(128)S(1)}, u32[32]{0:T(128)}, u32[]{:S(2)}) copy-start(u32[32]{0:T(128)} %constant.20) | copy-start | bytes 388
  0.7 14.2 %copy-start.12 = (s32[8]{0:T(128)S(1)}, s32[8]{0:T(128)}, u32[]{:S(2)}) copy-start(s32[8]{0:T(128)} %param.10) | copy-start | bytes 100
  0.7 14.2 %copy-start.11 = (f32[16]{0:T(128)S(1)}, f32[16]{0:T(128)}, u32[]{:S(2)}) copy-start(f32[16]{0:T(128)} %param.11) | copy-start | bytes 196
  1.6 15.7 %collective-permute-start = (f32[1,16,256]{1,2,0:T(8,128)S(1)}, f32[1,16,256]{1,2,0:T(8,128)S(1)}, u32[]{:S(2)}, u32[]{:S(2)}) collective-permute-start(f32[1,16,256]{1,2,0:T(8,128)S(1)} %get-tuple-element.54), channel_id=1, source_target_pairs={{0,4},{4,8},{8,12},{1,5},{5,9},{9,13},{2,6},{6,10},{10,14},{3,7},{... | collective-permute-start | bytes 49160 | tf_op jit(solution)/shard_map/ppermute | solution.py:23
  4.0 13.3 %collective-permute-start.1 = (f32[1,16,256]{1,2,0:T(8,128)S(1)}, f32[1,16,256]{1,2,0:T(8,128)S(1)}, u32[]{:S(2)}, u32[]{:S(2)}) collective-permute-start(f32[1,16,256]{1,2,0:T(8,128)S(1)} %get-tuple-element.54), channel_id=1, source_target_pairs={{4,0},{8,4},{12,8},{5,1},{9,5},{13,9},{6,2},{10,6},{14,10},{7,3},{... | collective-permute-start | bytes 49160 | tf_op jit(solution)/shard_map/ppermute | solution.py:26
  7.4 1.0 copy-start.4
  8.4 19.9 %collective-permute-start.4 = (f32[8,1,16,256]{3,2,1,0:T(8,128)S(1)}, f32[8,1,16,256]{3,2,1,0:T(8,128)S(1)}, u32[]{:S(2)}, u32[]{:S(2)}) collective-permute-start(f32[8,1,16,256]{3,2,1,0:T(8,128)S(1)} %get-tuple-element.19), channel_id=1, source_target_pairs={{0,4},{4,8},{8,12},{1,5},{5,9},{9,13},{2,6},{6,10},{10,14},{3,7},{... | collective-permute-start | bytes 393224 | tf_op jit(solution)/shard_map/ppermute | solution.py:23
  13.6 14.9 %collective-permute-start.5 = (f32[8,1,16,256]{3,2,1,0:T(8,128)S(1)}, f32[8,1,16,256]{3,2,1,0:T(8,128)S(1)}, u32[]{:S(2)}, u32[]{:S(2)}) collective-permute-start(f32[8,1,16,256]{3,2,1,0:T(8,128)S(1)} %get-tuple-element.18), channel_id=1, source_target_pairs={{4,0},{8,4},{12,8},{5,1},{9,5},{13,9},{6,2},{10,6},{14,10},{7,3},{... | collective-permute-start | bytes 393224 | tf_op jit(solution)/shard_map/ppermute | solution.py:26
  17.5 5.5 %collective-permute-start.2 = (f32[10,1,256]{2,1,0:T(1,128)S(1)}, f32[10,1,256]{2,1,0:T(1,128)S(1)}, u32[]{:S(2)}, u32[]{:S(2)}) collective-permute-start(f32[10,1,256]{2,1,0:T(1,128)S(1)} %get-tuple-element.46), channel_id=1, source_target_pairs={{0,1},{1,2},{2,3},{4,5},{5,6},{6,7},{8,9},{9,10},{10,11},{12,13},{... | collective-permute-start | bytes 30728 | tf_op jit(solution)/shard_map/ppermute | solution.py:23
  21.0 5.6 %collective-permute-start.3 = (f32[10,1,256]{2,1,0:T(1,128)S(1)}, f32[10,1,256]{2,1,0:T(1,128)S(1)}, u32[]{:S(2)}, u32[]{:S(2)}) collective-permute-start(f32[10,1,256]{2,1,0:T(1,128)S(1)} %get-tuple-element.47), channel_id=1, source_target_pairs={{1,0},{2,1},{3,2},{5,4},{6,5},{7,6},{9,8},{10,9},{11,10},{13,12},{... | collective-permute-start | bytes 30728 | tf_op jit(solution)/shard_map/ppermute | solution.py:26
  28.3 12.3 %copy-start.6 = (f32[8,16,256]{2,1,0:T(8,128)}, f32[8,16,256]{2,1,0:T(8,128)S(1)}, u32[]{:S(2)}) copy-start(f32[8,16,256]{2,1,0:T(8,128)S(1)} %get-tuple-element.25) | copy-start | bytes 393220
  28.3 12.3 %copy-start.7 = (f32[8,16,256]{2,1,0:T(8,128)}, f32[8,16,256]{2,1,0:T(8,128)S(1)}, u32[]{:S(2)}) copy-start(f32[8,16,256]{2,1,0:T(8,128)S(1)} %get-tuple-element.26) | copy-start | bytes 393220
  28.3 12.2 %copy-start.8 = (f32[8,1,16,256]{3,2,1,0:T(8,128)}, f32[8,1,16,256]{3,2,1,0:T(8,128)S(1)}, u32[]{:S(2)}) copy-start(f32[8,1,16,256]{3,2,1,0:T(8,128)S(1)} %collective-permute-done.4) | copy-start | bytes 393220
  28.5 12.1 %copy-start.9 = (f32[8,1,16,256]{3,2,1,0:T(8,128)}, f32[8,1,16,256]{3,2,1,0:T(8,128)S(1)}, u32[]{:S(2)}) copy-start(f32[8,1,16,256]{3,2,1,0:T(8,128)S(1)} %collective-permute-done.5) | copy-start | bytes 393220
  28.5 12.0 %copy-start.3 = (f32[8,10,16,256]{3,2,1,0:T(8,128)}, f32[8,10,16,256]{3,2,1,0:T(8,128)S(1)}, u32[]{:S(2)}) copy-start(f32[8,10,16,256]{3,2,1,0:T(8,128)S(1)} %constant_dynamic-update-slice_fusion) | copy-start | bytes 3932164
  28.6 6.3 %collective-permute-start.6 = (f32[8,10,1,256]{3,2,1,0:T(1,128)S(1)}, f32[8,10,1,256]{3,2,1,0:T(1,128)S(1)}, u32[]{:S(2)}, u32[]{:S(2)}) collective-permute-start(f32[8,10,1,256]{3,2,1,0:T(1,128)S(1)} %get-tuple-element.14), channel_id=1, source_target_pairs={{0,1},{1,2},{2,3},{4,5},{5,6},{6,7},{8,9},{9,10},{10,11},{12,13},{... | collective-permute-start | bytes 245768 | tf_op jit(solution)/shard_map/ppermute | solution.py:23
  32.1 6.9 %collective-permute-start.7 = (f32[8,10,1,256]{3,2,1,0:T(1,128)S(1)}, f32[8,10,1,256]{3,2,1,0:T(1,128)S(1)}, u32[]{:S(2)}, u32[]{:S(2)}) collective-permute-start(f32[8,10,1,256]{3,2,1,0:T(1,128)S(1)} %get-tuple-element.15), channel_id=1, source_target_pairs={{1,0},{2,1},{3,2},{5,4},{6,5},{7,6},{9,8},{10,9},{11,10},{13,12},{... | collective-permute-start | bytes 245768 | tf_op jit(solution)/shard_map/ppermute | solution.py:26
  39.0 1.5 %copy-start.10 = (f32[8,10,1,256]{3,2,1,0:T(1,128)}, f32[8,10,1,256]{3,2,1,0:T(1,128)S(1)}, u32[]{:S(2)}) copy-start(f32[8,10,1,256]{3,2,1,0:T(1,128)S(1)} %collective-permute-done.7) | copy-start | bytes 245764
  40.6 27.1 %copy-start.5 = (f32[8,16,256]{2,1,0:T(8,128)S(1)}, f32[8,16,256]{2,1,0:T(8,128)}, u32[]{:S(2)}) copy-start(f32[8,16,256]{2,1,0:T(8,128)} %param.7) | copy-start | bytes 393220
  50.3 34.7 %copy-start.1 = (f32[8,8,16,256]{3,2,1,0:T(8,128)}, f32[8,8,16,256]{3,2,1,0:T(8,128)S(1)}, u32[]{:S(2)}) copy-start(f32[8,8,16,256]{3,2,1,0:T(8,128)S(1)} %get-tuple-element.9) | copy-start | bytes 3145732
  68.8 1.0 copy-start.2
  86.6 3.6 %collective-permute-start.8 = (f32[8,1,16,256]{3,2,1,0:T(8,128)S(1)}, f32[8,1,16,256]{3,2,1,0:T(8,128)S(1)}, u32[]{:S(2)}, u32[]{:S(2)}) collective-permute-start(f32[8,1,16,256]{3,2,1,0:T(8,128)S(1)} %get-tuple-element.16), channel_id=1, source_target_pairs={{0,4},{4,8},{8,12},{1,5},{5,9},{9,13},{2,6},{6,10},{10,14},{3,7},{... | collective-permute-start | bytes 393224 | tf_op jit(solution)/shard_map/ppermute | solution.py:23
  88.9 4.7 %collective-permute-start.9 = (f32[8,1,16,256]{3,2,1,0:T(8,128)S(1)}, f32[8,1,16,256]{3,2,1,0:T(8,128)S(1)}, u32[]{:S(2)}, u32[]{:S(2)}) collective-permute-start(f32[8,1,16,256]{3,2,1,0:T(8,128)S(1)} %get-tuple-element.17), channel_id=1, source_target_pairs={{4,0},{8,4},{12,8},{5,1},{9,5},{13,9},{6,2},{10,6},{14,10},{7,3},{... | collective-permute-start | bytes 393224 | tf_op jit(solution)/shard_map/ppermute | solution.py:26
  93.7 5.5 %collective-permute-start.10 = (f32[8,10,1,256]{3,2,1,0:T(1,128)S(1)}, f32[8,10,1,256]{3,2,1,0:T(1,128)S(1)}, u32[]{:S(2)}, u32[]{:S(2)}) collective-permute-start(f32[8,10,1,256]{3,2,1,0:T(1,128)S(1)} %get-tuple-element.12), channel_id=1, source_target_pairs={{0,1},{1,2},{2,3},{4,5},{5,6},{6,7},{8,9},{9,10},{10,11},{12,13},{... | collective-permute-start | bytes 245768 | tf_op jit(solution)/shard_map/ppermute | solution.py:23
  97.2 6.3 %collective-permute-start.11 = (f32[8,10,1,256]{3,2,1,0:T(1,128)S(1)}, f32[8,10,1,256]{3,2,1,0:T(1,128)S(1)}, u32[]{:S(2)}, u32[]{:S(2)}) collective-permute-start(f32[8,10,1,256]{3,2,1,0:T(1,128)S(1)} %get-tuple-element.13), channel_id=1, source_target_pairs={{1,0},{2,1},{3,2},{5,4},{6,5},{7,6},{9,8},{10,9},{11,10},{13,12},{... | collective-permute-start | bytes 245768 | tf_op jit(solution)/shard_map/ppermute | solution.py:26
